TPU v7x, 32 devices: a whole 2x2x4 slice. The times are simulated.
32 devices in a mesh: grp: 2 (over y), slab: 4 (over z), orb: 2 (over x), rep: 2 (over core).
Axes of the slice: x: 2, y: 2, z: 4, core: 2. Of those that a mesh axis runs over, the one named last changes fastest.
Arguments:
- orbitals: bfloat16 [16, 32, 1024], P(('grp', 'slab', 'orb')), parts along dimension 0, may hold values from -6 to 6
- corners: int32 [16, 3], P('grp'), parts along dimension 0, may hold values from 0 to 191, as said below
- partners: int32 [16, 24], P(('grp', 'slab', 'orb')), parts along dimension 0, may hold values from -1 to 7, as said below
- kernel: float32 [32, 1024], replicated, may hold values from 0.05 to 5
Outputs:
- exchange_boxes: float32 [16, 32, 1024], P(('grp', 'slab', 'orb')), parts along dimension 0
- exchange_energy: float32 [2], P('grp'), parts along dimension 0
There are 2 independent parts, one for each index of `grp`. A program takes and returns all parts, laid end to end along the dimension named above; an argument that names none is the same for every part. Nothing has to cross between parts.
Inputs may be any that keep to these rules, and one draw needn't show every extreme that they name: corners[i, 2] lies in the slab of orbital i: from 12 * (i // (1 * 2)) to 12 more less one; corners[i, 0] and corners[i, 1] lie below 192. `partners`: row i starts with i itself, names distinct orbitals whose boxes intersect box i (every component of o is above -32 and below 32), and has its -1 entries only after all others.
All inputs are finite; a program needn't handle non-finite values.
Results may differ from a plain program's by a relative error of at most 0.0003.
Values may be sent and summed in bfloat16 or wider, within the bound.
A program may use at most 64 MiB of HBM per device.

v0:
```python
import math
import jax
import jax.numpy as jnp
from jax import lax
from jax.sharding import PartitionSpec as P

G = 192
ZDEV = 12
PB = 4


def passed_along(array, axis, by):
    size = lax.axis_size(axis)
    return lax.ppermute(array, axis, [(i, (i + by) % size) for i in range(size)])


def wrapped(deltas, lengths):
    halfway = lengths // 2
    return jnp.mod(deltas + halfway, lengths) - halfway


def edge_shifter(offsets, box_edge):
    row_ids = lax.broadcasted_iota(jnp.int32, (offsets.shape[0], box_edge, box_edge), 1)
    col_ids = lax.broadcasted_iota(jnp.int32, (offsets.shape[0], box_edge, box_edge), 2)
    return (col_ids == row_ids + offsets[:, None, None]).astype(jnp.bfloat16)


def plane_shifter(offsets_b, offsets_c, box_edge):
    plane = box_edge * box_edge
    source = lax.broadcasted_iota(jnp.int32, (offsets_b.shape[0], plane, plane), 1)
    target = lax.broadcasted_iota(jnp.int32, (offsets_b.shape[0], plane, plane), 2)
    match_b = source // box_edge == target // box_edge + offsets_b[:, None, None]
    match_c = jnp.mod(source, box_edge) == jnp.mod(target, box_edge) + offsets_c[:, None, None]
    return (match_b & match_c).astype(jnp.bfloat16)


def place_boxes(orbital_boxes, offsets, box_edge):
    stride_along_first = edge_shifter(offsets[:, 0], box_edge)
    displaced_density = jnp.einsum(
        "rkd,rdw->rkw", stride_along_first, orbital_boxes, preferred_element_type=jnp.float32
    ).astype(jnp.bfloat16)
    step_plane = plane_shifter(offsets[:, 1], offsets[:, 2], box_edge)
    return jnp.einsum(
        "pam,pmn->pan", displaced_density, step_plane, preferred_element_type=jnp.float32
    )


def fourier_tables(box_edge):
    grid_ids = jnp.arange(box_edge, dtype=jnp.int32)
    phases = jnp.mod(grid_ids[:, None] * grid_ids[None, :], box_edge)
    angles = phases.astype(jnp.float32) * (2.0 * math.pi / box_edge)
    plane_ids = jnp.arange(box_edge * box_edge, dtype=jnp.int32)
    outer_ids = plane_ids // box_edge
    inner_ids = jnp.mod(plane_ids, box_edge)
    plane_phases = jnp.mod(
        outer_ids[:, None] * outer_ids[None, :] + inner_ids[:, None] * inner_ids[None, :], box_edge
    )
    plane_angles = plane_phases.astype(jnp.float32) * (2.0 * math.pi / box_edge)
    return (jnp.cos(angles), jnp.sin(angles), jnp.cos(plane_angles), jnp.sin(plane_angles))


def edge_rotation(values, matrix):
    return jnp.einsum("ka,pam->pkm", matrix, values, precision=lax.Precision.HIGHEST)


def plane_turn(values, table):
    return jnp.einsum("pam,mn->pan", values, table, precision=lax.Precision.HIGHEST)


def poisson(density, kernel, tables):
    cosine, sine, plane_cos, plane_sin = tables
    plane_real = plane_turn(density, plane_cos)
    plane_imag = -plane_turn(density, plane_sin)
    real_part = edge_rotation(plane_real, cosine) + edge_rotation(plane_imag, sine)
    imag_part = edge_rotation(plane_imag, cosine) - edge_rotation(plane_real, sine)
    real_part = real_part * kernel[None]
    imag_part = imag_part * kernel[None]
    back_real = edge_rotation(real_part, cosine) - edge_rotation(imag_part, sine)
    back_imag = edge_rotation(imag_part, cosine) + edge_rotation(real_part, sine)
    result = plane_turn(back_real, plane_cos) - plane_turn(back_imag, plane_sin)
    box_edge = density.shape[1]
    return result / float(box_edge**3)


def body(orbitals, corners, partners, kernel):
    own_count = orbitals.shape[0]
    box_edge = orbitals.shape[1]
    plane = box_edge * box_edge
    slab_count = lax.axis_size("slab")
    orb_count = lax.axis_size("orb")
    group_size = own_count * orb_count
    slab_position = lax.axis_index("slab")
    halo_depth = (ZDEV + box_edge - 2) // ZDEV
    gathered = lax.all_gather(orbitals, "orb", axis=0, tiled=True)
    lower = [gathered]
    upper = [gathered]
    for _ in range(halo_depth):
        lower.append(passed_along(lower[-1], "slab", 1))
        upper.append(passed_along(upper[-1], "slab", -1))
    nearby = jnp.concatenate(lower[::-1] + upper[1:], axis=0)
    rep_count = lax.axis_size("rep")
    rep_index = lax.axis_index("rep")
    half_slots = partners.shape[1] // rep_count
    chosen = lax.dynamic_index_in_dim(
        partners.reshape(own_count, half_slots, rep_count), rep_index, 2, keepdims=False
    )
    first_own = (slab_position * orb_count + lax.axis_index("orb")) * own_count
    owner_ids = jnp.repeat(jnp.arange(own_count, dtype=jnp.int32), half_slots)
    flat_ids = chosen.reshape(own_count * half_slots)
    usable = (flat_ids >= 0).astype(jnp.float32)
    safe_ids = jnp.maximum(flat_ids, 0)
    neighbour_slab = safe_ids // group_size
    slab_step = jnp.mod(neighbour_slab - slab_position + halo_depth, slab_count) - halo_depth
    pool_rows = (slab_step + halo_depth) * group_size + jnp.mod(safe_ids, group_size)
    lengths = jnp.array([G, G, ZDEV * slab_count], jnp.int32)
    own_corners = jnp.take(corners, first_own + owner_ids, axis=0, mode="clip")
    partner_corners = jnp.take(corners, safe_ids, axis=0, mode="clip")
    offsets = wrapped(own_corners - partner_corners, lengths)
    tables = fourier_tables(box_edge)
    block_size = PB
    block_count = own_count * half_slots // block_size

    def block_work(block_index, carry):
        exchange, energy = carry
        first_pair = block_index * block_size
        owner_slot = first_pair // half_slots
        slots = lax.dynamic_slice_in_dim(pool_rows, first_pair, block_size)
        block_offsets = lax.dynamic_slice_in_dim(offsets, first_pair, block_size, 0)
        block_usable = lax.dynamic_slice_in_dim(usable, first_pair, block_size)

        def active(anchor):
            orbital_boxes = jnp.take(nearby, slots, axis=0, mode="clip")
            shifted = (
                place_boxes(orbital_boxes, block_offsets, box_edge) * block_usable[:, None, None]
            )
            centre = lax.dynamic_index_in_dim(orbitals, owner_slot, 0, keepdims=False).astype(
                jnp.float32
            )
            density = centre[None] * shifted
            potential = poisson(density, kernel, tables)
            return (jnp.sum(potential * shifted, axis=0), jnp.sum(density * potential))

        def skipped(anchor):
            return (jnp.zeros((box_edge, plane), jnp.float32), jnp.zeros((), jnp.float32))

        pair_term, energy_part = lax.cond(jnp.sum(block_usable) > 0.0, active, skipped, first_pair)
        previous = lax.dynamic_index_in_dim(exchange, owner_slot, 0, keepdims=False)
        exchange = lax.dynamic_update_index_in_dim(exchange, previous - pair_term, owner_slot, 0)
        return (exchange, energy + energy_part)

    start_state = (jnp.zeros((own_count, box_edge, plane), jnp.float32), jnp.zeros((), jnp.float32))
    exchange, energy = lax.fori_loop(0, block_count, block_work, start_state)
    exchange_total, replica_energy = lax.psum((exchange, energy), "rep")
    energy_all = lax.psum(replica_energy, ("slab", "orb"))
    orbital_total = own_count * slab_count * orb_count
    exchange_energy = -energy_all / (2.0 * orbital_total * box_edge**3)
    return (exchange_total, exchange_energy.reshape(1))


def solution(mesh):
    in_specs = (
        P(("grp", "slab", "orb"), None, None),
        P("grp", None),
        P(("grp", "slab", "orb"), None),
        P(),
    )
    out_specs = (P(("grp", "slab", "orb"), None, None), P("grp"))
    return jax.shard_map(body, mesh=mesh, in_specs=in_specs, out_specs=out_specs, check_vma=False)
```

profile of v0, /device:TPU:0, one launch (start us, length us, event | category | flops | bytes accessed | tf_op | source)
XLA Modules:
  0.0 167.7 jit_solution(17566683294554462132)
XLA Ops:
  7.2 6.1 %all_gather.3 = bf16[2,32,1024]{2,1,0:T(8,128)(2,1)S(1)} all-gather(bf16[1,32,1024]{2,1,0:T(8,128)(2,1)} %param.9), channel_id=1, replica_groups=mesh['grp'=2,'slab'=4,'orb'=2,'rep'=2] {'orb'}, dimensions={0}, use_global_device_ids=true | all-gather | bytes 196608 | tf_op jit(solution)/shard_map/all_gather | solution.py:94
  13.3 2.1 %collective-permute-start = (bf16[2,32,1024]{2,1,0:T(8,128)(2,1)S(1)}, bf16[2,32,1024]{2,1,0:T(8,128)(2,1)S(1)}, u32[]{:S(2)}, u32[]{:S(2)}) collective-permute-start(bf16[2,32,1024]{2,1,0:T(8,128)(2,1)S(1)} %all_gather.3), channel_id=1, source_target_pairs={{0,4},{4,8},{8,12},{12,0},{1,5},{5,9},{9,13},{13,1},{2,6},{6,10},{... | collective-permute-start | bytes 393224 | tf_op jit(solution)/shard_map/ppermute | solution.py:14
  15.4 2.0 %collective-permute-start.3 = (bf16[2,32,1024]{2,1,0:T(8,128)(2,1)S(1)}, bf16[2,32,1024]{2,1,0:T(8,128)(2,1)S(1)}, u32[]{:S(2)}, u32[]{:S(2)}) collective-permute-start(bf16[2,32,1024]{2,1,0:T(8,128)(2,1)S(1)} %all_gather.3), channel_id=1, source_target_pairs={{0,12},{4,0},{8,4},{12,8},{1,13},{5,1},{9,5},{13,9},{2,14},{6,2},{... | collective-permute-start | bytes 393224 | tf_op jit(solution)/shard_map/ppermute | solution.py:14
  17.4 0.8 copy.13
  18.7 1.3 reduce.13
  21.7 0.8 fusion.67
  22.6 3.9 %collective-permute-start.4 = (bf16[2,32,1024]{2,1,0:T(8,128)(2,1)S(1)}, bf16[2,32,1024]{2,1,0:T(8,128)(2,1)S(1)}, u32[]{:S(2)}, u32[]{:S(2)}) collective-permute-start(bf16[2,32,1024]{2,1,0:T(8,128)(2,1)S(1)} %collective-permute-done.3), channel_id=1, source_target_pairs={{0,12},{4,0},{8,4},{12,8},{1,13},{5,1},{9,5},{13,9},{2,14},{6,2},{... | collective-permute-start | bytes 393224 | tf_op jit(solution)/shard_map/ppermute | solution.py:14
  26.4 2.5 %collective-permute-done.1 = bf16[2,32,1024]{2,1,0:T(8,128)(2,1)S(1)} collective-permute-done((bf16[2,32,1024]{2,1,0:T(8,128)(2,1)S(1)}, bf16[2,32,1024]{2,1,0:T(8,128)(2,1)S(1)}, u32[]{:S(2)}, u32[]{:S(2)}) %collective-permute-start.1) | collective-permute-done | bytes 131104 | tf_op jit(solution)/shard_map/ppermute | solution.py:14
  29.2 4.9 %collective-permute-start.5 = (bf16[2,32,1024]{2,1,0:T(8,128)(2,1)S(1)}, bf16[2,32,1024]{2,1,0:T(8,128)(2,1)S(1)}, u32[]{:S(2)}, u32[]{:S(2)}) collective-permute-start(bf16[2,32,1024]{2,1,0:T(8,128)(2,1)S(1)} %collective-permute-done.4), channel_id=1, source_target_pairs={{0,12},{4,0},{8,4},{12,8},{1,13},{5,1},{9,5},{13,9},{2,14},{6,2},{... | collective-permute-start | bytes 393224 | tf_op jit(solution)/shard_map/ppermute | solution.py:14
  34.1 2.7 %collective-permute-done.2 = bf16[2,32,1024]{2,1,0:T(8,128)(2,1)S(1)} collective-permute-done((bf16[2,32,1024]{2,1,0:T(8,128)(2,1)S(1)}, bf16[2,32,1024]{2,1,0:T(8,128)(2,1)S(1)}, u32[]{:S(2)}, u32[]{:S(2)}) %collective-permute-start.2) | collective-permute-done | bytes 131104 | tf_op jit(solution)/shard_map/ppermute | solution.py:14
  37.3 93.5 %while.20 = (s32[]{:T(128)}, f32[1,32,1024]{2,1,0:T(8,128)S(1)}, f32[]{:T(128)}, f32[12]{0:T(128)S(1)}, bf16[1,32,1024]{2,1,0:T(8,128)(2,1)}, /*index=5*/s32[12,...) while((s32[]{:T(128)}, f32[1,32,1024]{2,1,0:T(8,128)S(1)}, ...), condition=%wide.region_6.7_spmd.clone.clone.clone, body=%wide.region_0.6_spmd.clone.clone.clone.sunk | while | flops 7178883072 | bytes 56513292 | solution.py:152
  37.4 0.8 fusion.96
  38.8 3.7 %fusion.97 = f32[1024,1024]{1,0:T(8,128)} fusion(s32[1024]{0:T(1024)S(1)} %get-tuple-element.785, s32[1024]{0:T(1024)S(1)} %get-tuple-element.784), kind=kLoop, calls=%fused_computation.81.clone.1 | loop fusion | flops 16777216 | bytes 4202496 | tf_op jit(solution)/shard_map/mul | solution.py:58
  42.5 77.8 %conditional.5 = (f32[32,1024]{1,0:T(8,128)S(1)}, f32[]{:T(128)}) conditional(s32[]{:T(128)} %convert_element_type.98, () %tuple.97, (bf16[1,32,1024]{2,1,0:T(8,128)(2,1)S(1)}, s32[12,3]{0,1:T(4,128)S(1)}, s32[]{:T(128)}, s32[12]{0:T(128)S(1)}, bf16[14,32,1024]{2,1,0:T(8,128)(2,1)S(1)}, /*index=5*/f32[4]{0:T(128)S(1)}, f32[1024,1024]{1,0:T(8,128)}, ...), branch_computations={%region_2.2_spmd, %region_3.5_spmd.clone} | conditional | flops 7162058752 | bytes 51126648 | solution.py:146
  43.3 4.2 %fusion.38 = f32[4,32,1024]{2,1,0:T(8,128)S(1)} fusion(s32[4]{0:T(128)S(1)} %get-tuple-element.652, s32[1024]{0:T(1024)S(1)} %get-tuple-element.655, s32[1024]{0:T(1024)S(1)} %get-tuple-element.656, s32[4]{0:T(128)S(1)} %get-tuple-element.653, s32[1024]{0:T(1024)S(1)} %get-tuple-element.654, s32[1024]{0:T(1024)S(1)} %get-tuple-element.657, ...), kind=kOutput, calls=%fused_computation.44 | convolution fusion | flops 314843136 | bytes 804928 | tf_op jit(solution)/shard_map/while/body/eval_jaxpr/cond/branch_1_fun/pam,pmn->pan/dot_general | solution.py:43
  47.5 17.6 %fusion.31 = f32[4,32,1024]{2,1,0:T(8,128)S(1)} fusion(f32[1024,1024]{1,0:T(8,128)} %get-tuple-element.609, f32[4,32,1024]{2,1,0:T(8,128)S(1)} %fusion.38, f32[32,1024]{1,0:T(8,128)S(1)} %bitcast_convert_fusion), kind=kOutput, calls=%fused_computation.33 | convolution fusion | flops 1610874880 | bytes 5373952 | tf_op jit(solution)/shard_map/while/body/eval_jaxpr/cond/branch_1_fun/pam,mn->pan/dot_general | solution.py:67
  65.1 16.2 %fusion.26 = f32[4,32,1024]{2,1,0:T(8,128)S(1)} fusion(f32[1024,1024]{1,0:T(8,128)S(1)} %copy-done, f32[4,32,1024]{2,1,0:T(8,128)S(1)} %fusion.38, f32[32,1024]{1,0:T(8,128)S(1)} %bitcast_convert_fusion), kind=kOutput, calls=%fused_computation.28 | convolution fusion | flops 1610743808 | bytes 5373952 | tf_op jit(solution)/shard_map/while/body/eval_jaxpr/cond/branch_1_fun/pam,mn->pan/dot_general | solution.py:67
  86.7 16.2 %fusion.25 = f32[4,32,1024]{2,1,0:T(8,128)S(1)} fusion(f32[4,32,1024]{2,1,0:T(8,128)S(1)} %fusion.33, f32[1024,1024]{1,0:T(8,128)S(1)} %copy-done), kind=kOutput, calls=%fused_computation.27 | convolution fusion | flops 1610612736 | bytes 5242880 | tf_op jit(solution)/shard_map/while/body/eval_jaxpr/cond/branch_1_fun/pam,mn->pan/dot_general | solution.py:67
  102.9 16.7 %multiply_reduce_fusion = (f32[]{:T(128)}, f32[32,1024]{1,0:T(8,128)S(1)}) fusion(f32[4,32,1024]{2,1,0:T(8,128)S(1)} %fusion.38, f32[32,1024]{1,0:T(8,128)S(1)} %bitcast_convert_fusion, f32[4,32,1024]{2,1,0:T(8,128)S(1)} %fusion.25, f32[4,32,1024]{2,1,0:T(8,128)S(1)} %fusion.32, f32[1024,1024]{1,0:T(8,128)S(1)} %copy-done), kind=kOutput, calls=%fused_computation.46 | convolution fusion | flops 1611497472 | bytes 6029316 | tf_op jit(solution)/shard_map/while/body/eval_jaxpr/cond/branch_1_fun/pam,mn->pan/dot_general | solution.py:67
  121.8 3.7 %fusion.97 = f32[1024,1024]{1,0:T(8,128)} fusion(s32[1024]{0:T(1024)S(1)} %get-tuple-element.785, s32[1024]{0:T(1024)S(1)} %get-tuple-element.784), kind=kLoop, calls=%fused_computation.81.clone.1 | loop fusion | flops 16777216 | bytes 4202496 | tf_op jit(solution)/shard_map/mul | solution.py:58
  127.1 3.7 %fusion.97 = f32[1024,1024]{1,0:T(8,128)} fusion(s32[1024]{0:T(1024)S(1)} %get-tuple-element.785, s32[1024]{0:T(1024)S(1)} %get-tuple-element.784), kind=kLoop, calls=%fused_computation.81.clone.1 | loop fusion | flops 16777216 | bytes 4202496 | tf_op jit(solution)/shard_map/mul | solution.py:58
  131.5 3.7 %psum.22 = f32[]{:T(128)} all-reduce(f32[]{:T(128)} %get-tuple-element.447), channel_id=1, replica_groups=mesh['grp'=2,'slab'=4,'orb'=2,'rep'=2] {'rep'}, use_global_device_ids=true, to_apply=%region_8.9 | all-reduce | flops 1 | bytes 8 | tf_op jit(solution)/shard_map/psum | solution.py:153
  135.2 22.3 %psum.23 = f32[]{:T(128)} all-reduce(f32[]{:T(128)} %psum.22), channel_id=1, replica_groups=mesh['grp'=2,'slab'=4,'orb'=2,'rep'=2] {'slab','orb'}, use_global_device_ids=true, to_apply=%region_9.10 | all-reduce | flops 1 | bytes 8 | tf_op jit(solution)/shard_map/psum | solution.py:154
  158.2 1.6 copy.38
  (74 shorter events, 11.5 us)
Async XLA Ops:
  7.2 151.0 %all-reduce.2.cloned.1.call-start = ((), (), s32[]{:S(2)}) async-start(), calls=%async_computation | async-start | bytes 262144 | tf_op jit(solution)/shard_map/psum | solution.py:153
  13.3 8.3 %collective-permute-start = (bf16[2,32,1024]{2,1,0:T(8,128)(2,1)S(1)}, bf16[2,32,1024]{2,1,0:T(8,128)(2,1)S(1)}, u32[]{:S(2)}, u32[]{:S(2)}) collective-permute-start(bf16[2,32,1024]{2,1,0:T(8,128)(2,1)S(1)} %all_gather.3), channel_id=1, source_target_pairs={{0,4},{4,8},{8,12},{12,0},{1,5},{5,9},{9,13},{13,1},{2,6},{6,10},{... | collective-permute-start | bytes 393224 | tf_op jit(solution)/shard_map/ppermute | solution.py:14
  15.4 7.2 %collective-permute-start.3 = (bf16[2,32,1024]{2,1,0:T(8,128)(2,1)S(1)}, bf16[2,32,1024]{2,1,0:T(8,128)(2,1)S(1)}, u32[]{:S(2)}, u32[]{:S(2)}) collective-permute-start(bf16[2,32,1024]{2,1,0:T(8,128)(2,1)S(1)} %all_gather.3), channel_id=1, source_target_pairs={{0,12},{4,0},{8,4},{12,8},{1,13},{5,1},{9,5},{13,9},{2,14},{6,2},{... | collective-permute-start | bytes 393224 | tf_op jit(solution)/shard_map/ppermute | solution.py:14
  21.7 7.2 %collective-permute-start.1 = (bf16[2,32,1024]{2,1,0:T(8,128)(2,1)S(1)}, bf16[2,32,1024]{2,1,0:T(8,128)(2,1)S(1)}, u32[]{:S(2)}, u32[]{:S(2)}) collective-permute-start(bf16[2,32,1024]{2,1,0:T(8,128)(2,1)S(1)} %collective-permute-done), channel_id=1, source_target_pairs={{0,4},{4,8},{8,12},{12,0},{1,5},{5,9},{9,13},{13,1},{2,6},{6,10},{... | collective-permute-start | bytes 393224 | tf_op jit(solution)/shard_map/ppermute | solution.py:14
  22.6 6.7 %collective-permute-start.4 = (bf16[2,32,1024]{2,1,0:T(8,128)(2,1)S(1)}, bf16[2,32,1024]{2,1,0:T(8,128)(2,1)S(1)}, u32[]{:S(2)}, u32[]{:S(2)}) collective-permute-start(bf16[2,32,1024]{2,1,0:T(8,128)(2,1)S(1)} %collective-permute-done.3), channel_id=1, source_target_pairs={{0,12},{4,0},{8,4},{12,8},{1,13},{5,1},{9,5},{13,9},{2,14},{6,2},{... | collective-permute-start | bytes 393224 | tf_op jit(solution)/shard_map/ppermute | solution.py:14
  28.9 7.9 %collective-permute-start.2 = (bf16[2,32,1024]{2,1,0:T(8,128)(2,1)S(1)}, bf16[2,32,1024]{2,1,0:T(8,128)(2,1)S(1)}, u32[]{:S(2)}, u32[]{:S(2)}) collective-permute-start(bf16[2,32,1024]{2,1,0:T(8,128)(2,1)S(1)} %collective-permute-done.1), channel_id=1, source_target_pairs={{0,4},{4,8},{8,12},{12,0},{1,5},{5,9},{9,13},{13,1},{2,6},{6,10},{... | collective-permute-start | bytes 393224 | tf_op jit(solution)/shard_map/ppermute | solution.py:14
  29.2 8.0 %collective-permute-start.5 = (bf16[2,32,1024]{2,1,0:T(8,128)(2,1)S(1)}, bf16[2,32,1024]{2,1,0:T(8,128)(2,1)S(1)}, u32[]{:S(2)}, u32[]{:S(2)}) collective-permute-start(bf16[2,32,1024]{2,1,0:T(8,128)(2,1)S(1)} %collective-permute-done.4), channel_id=1, source_target_pairs={{0,12},{4,0},{8,4},{12,8},{1,13},{5,1},{9,5},{13,9},{2,14},{6,2},{... | collective-permute-start | bytes 393224 | tf_op jit(solution)/shard_map/ppermute | solution.py:14
  37.3 5.2 %copy-start.1 = (f32[32,1024]{1,0:T(8,128)S(1)}, f32[32,1024]{1,0:T(8,128)}, u32[]{:S(2)}) copy-start(f32[32,1024]{1,0:T(8,128)} %get-tuple-element.783) | copy-start | bytes 393220 | tf_op jit(solution)/shard_map/while
  37.3 5.2 %copy-start.3 = (bf16[1,32,1024]{2,1,0:T(8,128)(2,1)S(1)}, bf16[1,32,1024]{2,1,0:T(8,128)(2,1)}, u32[]{:S(2)}) copy-start(bf16[1,32,1024]{2,1,0:T(8,128)(2,1)} %get-tuple-element.779) | copy-start | bytes 196612 | tf_op jit(solution)/shard_map/while
  47.5 17.6 %copy-start = (f32[1024,1024]{1,0:T(8,128)S(1)}, f32[1024,1024]{1,0:T(8,128)}, u32[]{:S(2)}) copy-start(f32[1024,1024]{1,0:T(8,128)} %get-tuple-element.609) | copy-start | bytes 12582916 | tf_op jit(solution)/shard_map/while/body/eval_jaxpr/cond
  120.3 5.2 %copy-start.1 = (f32[32,1024]{1,0:T(8,128)S(1)}, f32[32,1024]{1,0:T(8,128)}, u32[]{:S(2)}) copy-start(f32[32,1024]{1,0:T(8,128)} %get-tuple-element.783) | copy-start | bytes 393220 | tf_op jit(solution)/shard_map/while
  120.3 5.2 %copy-start.3 = (bf16[1,32,1024]{2,1,0:T(8,128)(2,1)S(1)}, bf16[1,32,1024]{2,1,0:T(8,128)(2,1)}, u32[]{:S(2)}) copy-start(bf16[1,32,1024]{2,1,0:T(8,128)(2,1)} %get-tuple-element.779) | copy-start | bytes 196612 | tf_op jit(solution)/shard_map/while
  125.6 5.2 %copy-start.1 = (f32[32,1024]{1,0:T(8,128)S(1)}, f32[32,1024]{1,0:T(8,128)}, u32[]{:S(2)}) copy-start(f32[32,1024]{1,0:T(8,128)} %get-tuple-element.783) | copy-start | bytes 393220 | tf_op jit(solution)/shard_map/while
  125.6 5.2 %copy-start.3 = (bf16[1,32,1024]{2,1,0:T(8,128)(2,1)S(1)}, bf16[1,32,1024]{2,1,0:T(8,128)(2,1)}, u32[]{:S(2)}) copy-start(bf16[1,32,1024]{2,1,0:T(8,128)(2,1)} %get-tuple-element.779) | copy-start | bytes 196612 | tf_op jit(solution)/shard_map/while
  130.9 0.7 copy-start.2
Sparse Core Ops, SparseCore 0:
  131.7 19.1 all-reduce.1
where the time goes:
time: 168 us
  matrix products  76.2 us (45%)
  blocking collectives  32.1 us (19%)
  other arithmetic  16.2 us (10%)
  between operations  15.9 us (9%)
  starting transfers between devices  12.9 us (8%)
  local copies, waits for them, and re-layouts  5.64 us (3%)
  waiting for transfers between devices  5.57 us (3%)
  loops' own time  3.13 us (2%)
    dot_general x4, matrix products, plane_turn(): jnp.einsum('pam,mn->pan', values, table, precision=lax.Precision.HIGHEST)  66.7 us
    psum x1, blocking collectives, body(): energy_all = lax.psum(replica_energy, ('slab', 'orb'))  22.3 us
    ppermute x6, starting transfers between devices, passed_along(): lax.ppermute(array, axis, [(i, (i + by) % size) for i in range(size)])  12.9 us
    mul x3, other arithmetic, fourier_tables(): plane_angles = plane_phases.astype(jnp.float32) * (2.0 * math.pi / box_edge)  11 us
    all_gather x1, blocking collectives, body(): gathered = lax.all_gather(orbitals, 'orb', axis=0, tiled=True)  6.14 us
    ppermute x6, waiting for transfers between devices, passed_along(): lax.ppermute(array, axis, [(i, (i + by) % size) for i in range(size)])  5.54 us
    dot_general x8, matrix products, edge_rotation(): jnp.einsum('ka,pam->pkm', matrix, values, precision=lax.Precision.HIGHEST)  5.3 us
    dot_general x1, matrix products, place_boxes(): jnp.einsum('pam,pmn->pan', displaced_density, step_plane, preferred_eleme...  4.2 us
  transfers between devices with their start and end apart: 7, of which 4 were waited for; matrix products, arithmetic and copies ran while one was open for 3% of the time, Pallas kernels for 0%

commit v1 on v0

--- a/solution.py
+++ b/solution.py
@@ -151,7 +151,8 @@
     start_state = (jnp.zeros((own_count, box_edge, plane), jnp.float32), jnp.zeros((), jnp.float32))
     exchange, energy = lax.fori_loop(0, block_count, block_work, start_state)
     exchange_total, replica_energy = lax.psum((exchange, energy), "rep")
-    energy_all = lax.psum(replica_energy, ("slab", "orb"))
+    shards = lax.all_gather(replica_energy, ("slab", "orb"), axis=0, tiled=False)
+    energy_all = shards.sum(axis=0)
     orbital_total = own_count * slab_count * orb_count
     exchange_energy = -energy_all / (2.0 * orbital_total * box_edge**3)
     return (exchange_total, exchange_energy.reshape(1))

time: 168 us -> 170 us (1.012)
  local copies, waits for them, and re-layouts: 5.64 us -> 7.54 us
    psum x1 -> x0, blocking collectives: 22.3 us -> none  [body(): energy_all = lax.psum(replica_energy, ('slab', 'orb'))]
    unnamed x0 -> x1, blocking collectives: none -> 21.7 us
    unnamed x12 -> x17, local copies, waits for them, and re-layouts: 3.64 us -> 5.54 us
  transfers between devices with their start and end apart: 7 -> 7, of which waited for: 4 -> 4; matrix products, arithmetic and copies ran while one was open for 3% -> 5% of each run, Pallas kernels for 0% -> 0%
where the time goes in v1:
time: 170 us
  matrix products  76.2 us (45%)
  blocking collectives  31.4 us (18%)
  other arithmetic  16.8 us (10%)
  between operations  16 us (9%)
  starting transfers between devices  12.9 us (8%)
  local copies, waits for them, and re-layouts  7.54 us (4%)
  waiting for transfers between devices  5.58 us (3%)
  loops' own time  3.13 us (2%)
    dot_general x4, matrix products, plane_turn(): jnp.einsum('pam,mn->pan', values, table, precision=lax.Precision.HIGHEST)  66.7 us
    unnamed x1, blocking collectives  21.7 us
    ppermute x6, starting transfers between devices, passed_along(): lax.ppermute(array, axis, [(i, (i + by) % size) for i in range(size)])  12.9 us
    mul x3, other arithmetic, fourier_tables(): plane_angles = plane_phases.astype(jnp.float32) * (2.0 * math.pi / box_edge)  11 us
    all_gather x1, blocking collectives, body(): gathered = lax.all_gather(orbitals, 'orb', axis=0, tiled=True)  6.14 us
    unnamed x17, local copies, waits for them, and re-layouts  5.54 us
    ppermute x6, waiting for transfers between devices, passed_along(): lax.ppermute(array, axis, [(i, (i + by) % size) for i in range(size)])  5.54 us
    dot_general x8, matrix products, edge_rotation(): jnp.einsum('ka,pam->pkm', matrix, values, precision=lax.Precision.HIGHEST)  5.3 us
  transfers between devices with their start and end apart: 7, of which 4 were waited for; matrix products, arithmetic and copies ran while one was open for 5% of the time, Pallas kernels for 0%

profile of v1, /device:TPU:0, one launch (start us, length us, event | category | flops | bytes accessed | tf_op | source)
XLA Modules:
  0.0 169.6 jit_solution(17511443994075038303)
XLA Ops:
  7.2 6.1 %all_gather.9 = bf16[2,32,1024]{2,1,0:T(8,128)(2,1)S(1)} all-gather(bf16[1,32,1024]{2,1,0:T(8,128)(2,1)} %param.9), channel_id=1, replica_groups=mesh['grp'=2,'slab'=4,'orb'=2,'rep'=2] {'orb'}, dimensions={0}, use_global_device_ids=true | all-gather | bytes 196608 | tf_op jit(solution)/shard_map/all_gather | solution.py:94
  13.3 2.1 %collective-permute-start = (bf16[2,32,1024]{2,1,0:T(8,128)(2,1)S(1)}, bf16[2,32,1024]{2,1,0:T(8,128)(2,1)S(1)}, u32[]{:S(2)}, u32[]{:S(2)}) collective-permute-start(bf16[2,32,1024]{2,1,0:T(8,128)(2,1)S(1)} %all_gather.9), channel_id=1, source_target_pairs={{0,4},{4,8},{8,12},{12,0},{1,5},{5,9},{9,13},{13,1},{2,6},{6,10},{... | collective-permute-start | bytes 393224 | tf_op jit(solution)/shard_map/ppermute | solution.py:14
  15.4 2.0 %collective-permute-start.3 = (bf16[2,32,1024]{2,1,0:T(8,128)(2,1)S(1)}, bf16[2,32,1024]{2,1,0:T(8,128)(2,1)S(1)}, u32[]{:S(2)}, u32[]{:S(2)}) collective-permute-start(bf16[2,32,1024]{2,1,0:T(8,128)(2,1)S(1)} %all_gather.9), channel_id=1, source_target_pairs={{0,12},{4,0},{8,4},{12,8},{1,13},{5,1},{9,5},{13,9},{2,14},{6,2},{... | collective-permute-start | bytes 393224 | tf_op jit(solution)/shard_map/ppermute | solution.py:14
  17.4 0.8 copy.13
  18.7 1.3 reduce.14
  21.7 0.8 fusion.67
  22.6 3.9 %collective-permute-start.4 = (bf16[2,32,1024]{2,1,0:T(8,128)(2,1)S(1)}, bf16[2,32,1024]{2,1,0:T(8,128)(2,1)S(1)}, u32[]{:S(2)}, u32[]{:S(2)}) collective-permute-start(bf16[2,32,1024]{2,1,0:T(8,128)(2,1)S(1)} %collective-permute-done.3), channel_id=1, source_target_pairs={{0,12},{4,0},{8,4},{12,8},{1,13},{5,1},{9,5},{13,9},{2,14},{6,2},{... | collective-permute-start | bytes 393224 | tf_op jit(solution)/shard_map/ppermute | solution.py:14
  26.4 2.5 %collective-permute-done.1 = bf16[2,32,1024]{2,1,0:T(8,128)(2,1)S(1)} collective-permute-done((bf16[2,32,1024]{2,1,0:T(8,128)(2,1)S(1)}, bf16[2,32,1024]{2,1,0:T(8,128)(2,1)S(1)}, u32[]{:S(2)}, u32[]{:S(2)}) %collective-permute-start.1) | collective-permute-done | bytes 131104 | tf_op jit(solution)/shard_map/ppermute | solution.py:14
  29.2 4.9 %collective-permute-start.5 = (bf16[2,32,1024]{2,1,0:T(8,128)(2,1)S(1)}, bf16[2,32,1024]{2,1,0:T(8,128)(2,1)S(1)}, u32[]{:S(2)}, u32[]{:S(2)}) collective-permute-start(bf16[2,32,1024]{2,1,0:T(8,128)(2,1)S(1)} %collective-permute-done.4), channel_id=1, source_target_pairs={{0,12},{4,0},{8,4},{12,8},{1,13},{5,1},{9,5},{13,9},{2,14},{6,2},{... | collective-permute-start | bytes 393224 | tf_op jit(solution)/shard_map/ppermute | solution.py:14
  34.1 2.7 %collective-permute-done.2 = bf16[2,32,1024]{2,1,0:T(8,128)(2,1)S(1)} collective-permute-done((bf16[2,32,1024]{2,1,0:T(8,128)(2,1)S(1)}, bf16[2,32,1024]{2,1,0:T(8,128)(2,1)S(1)}, u32[]{:S(2)}, u32[]{:S(2)}) %collective-permute-start.2) | collective-permute-done | bytes 131104 | tf_op jit(solution)/shard_map/ppermute | solution.py:14
  37.3 93.5 %while.20 = (s32[]{:T(128)}, f32[1,32,1024]{2,1,0:T(8,128)S(1)}, f32[]{:T(128)}, f32[12]{0:T(128)S(1)}, bf16[1,32,1024]{2,1,0:T(8,128)(2,1)}, /*index=5*/s32[12,...) while((s32[]{:T(128)}, f32[1,32,1024]{2,1,0:T(8,128)S(1)}, ...), condition=%wide.region_6.7_spmd.clone.clone.clone, body=%wide.region_0.6_spmd.clone.clone.clone.sunk | while | flops 7178883072 | bytes 56513292 | solution.py:152
  38.8 3.7 %fusion.97 = f32[1024,1024]{1,0:T(8,128)} fusion(s32[1024]{0:T(1024)S(1)} %get-tuple-element.785, s32[1024]{0:T(1024)S(1)} %get-tuple-element.784), kind=kLoop, calls=%fused_computation.81.clone.1 | loop fusion | flops 16777216 | bytes 4202496 | tf_op jit(solution)/shard_map/mul | solution.py:58
  42.5 77.8 %conditional.5 = (f32[32,1024]{1,0:T(8,128)S(1)}, f32[]{:T(128)}) conditional(s32[]{:T(128)} %convert_element_type.98, () %tuple.97, (bf16[1,32,1024]{2,1,0:T(8,128)(2,1)S(1)}, s32[12,3]{0,1:T(4,128)S(1)}, s32[]{:T(128)}, s32[12]{0:T(128)S(1)}, bf16[14,32,1024]{2,1,0:T(8,128)(2,1)S(1)}, /*index=5*/f32[4]{0:T(128)S(1)}, f32[1024,1024]{1,0:T(8,128)}, ...), branch_computations={%region_2.2_spmd, %region_3.5_spmd.clone} | conditional | flops 7162058752 | bytes 51126648 | solution.py:146
  43.3 4.2 %fusion.38 = f32[4,32,1024]{2,1,0:T(8,128)S(1)} fusion(s32[4]{0:T(128)S(1)} %get-tuple-element.652, s32[1024]{0:T(1024)S(1)} %get-tuple-element.655, s32[1024]{0:T(1024)S(1)} %get-tuple-element.656, s32[4]{0:T(128)S(1)} %get-tuple-element.653, s32[1024]{0:T(1024)S(1)} %get-tuple-element.654, s32[1024]{0:T(1024)S(1)} %get-tuple-element.657, ...), kind=kOutput, calls=%fused_computation.44 | convolution fusion | flops 314843136 | bytes 804928 | tf_op jit(solution)/shard_map/while/body/eval_jaxpr/cond/branch_1_fun/pam,pmn->pan/dot_general | solution.py:43
  47.5 17.6 %fusion.31 = f32[4,32,1024]{2,1,0:T(8,128)S(1)} fusion(f32[1024,1024]{1,0:T(8,128)} %get-tuple-element.609, f32[4,32,1024]{2,1,0:T(8,128)S(1)} %fusion.38, f32[32,1024]{1,0:T(8,128)S(1)} %bitcast_convert_fusion), kind=kOutput, calls=%fused_computation.33 | convolution fusion | flops 1610874880 | bytes 5373952 | tf_op jit(solution)/shard_map/while/body/eval_jaxpr/cond/branch_1_fun/pam,mn->pan/dot_general | solution.py:67
  65.2 16.2 %fusion.26 = f32[4,32,1024]{2,1,0:T(8,128)S(1)} fusion(f32[1024,1024]{1,0:T(8,128)S(1)} %copy-done, f32[4,32,1024]{2,1,0:T(8,128)S(1)} %fusion.38, f32[32,1024]{1,0:T(8,128)S(1)} %bitcast_convert_fusion), kind=kOutput, calls=%fused_computation.28 | convolution fusion | flops 1610743808 | bytes 5373952 | tf_op jit(solution)/shard_map/while/body/eval_jaxpr/cond/branch_1_fun/pam,mn->pan/dot_general | solution.py:67
  86.7 16.2 %fusion.25 = f32[4,32,1024]{2,1,0:T(8,128)S(1)} fusion(f32[4,32,1024]{2,1,0:T(8,128)S(1)} %fusion.33, f32[1024,1024]{1,0:T(8,128)S(1)} %copy-done), kind=kOutput, calls=%fused_computation.27 | convolution fusion | flops 1610612736 | bytes 5242880 | tf_op jit(solution)/shard_map/while/body/eval_jaxpr/cond/branch_1_fun/pam,mn->pan/dot_general | solution.py:67
  102.9 16.7 %multiply_reduce_fusion = (f32[]{:T(128)}, f32[32,1024]{1,0:T(8,128)S(1)}) fusion(f32[4,32,1024]{2,1,0:T(8,128)S(1)} %fusion.38, f32[32,1024]{1,0:T(8,128)S(1)} %bitcast_convert_fusion, f32[4,32,1024]{2,1,0:T(8,128)S(1)} %fusion.25, f32[4,32,1024]{2,1,0:T(8,128)S(1)} %fusion.32, f32[1024,1024]{1,0:T(8,128)S(1)} %copy-done), kind=kOutput, calls=%fused_computation.46 | convolution fusion | flops 1611497472 | bytes 6029316 | tf_op jit(solution)/shard_map/while/body/eval_jaxpr/cond/branch_1_fun/pam,mn->pan/dot_general | solution.py:67
  121.9 3.7 %fusion.97 = f32[1024,1024]{1,0:T(8,128)} fusion(s32[1024]{0:T(1024)S(1)} %get-tuple-element.785, s32[1024]{0:T(1024)S(1)} %get-tuple-element.784), kind=kLoop, calls=%fused_computation.81.clone.1 | loop fusion | flops 16777216 | bytes 4202496 | tf_op jit(solution)/shard_map/mul | solution.py:58
  127.1 3.7 %fusion.97 = f32[1024,1024]{1,0:T(8,128)} fusion(s32[1024]{0:T(1024)S(1)} %get-tuple-element.785, s32[1024]{0:T(1024)S(1)} %get-tuple-element.784), kind=kLoop, calls=%fused_computation.81.clone.1 | loop fusion | flops 16777216 | bytes 4202496 | tf_op jit(solution)/shard_map/mul | solution.py:58
  132.2 3.6 %psum.15 = f32[1]{0:T(128)} all-reduce(f32[1]{0:T(128)} %bitcast.20), channel_id=1, replica_groups=mesh['grp'=2,'slab'=4,'orb'=2,'rep'=2] {'rep'}, use_global_device_ids=true, to_apply=%region_8.9 | all-reduce | flops 1 | bytes 8 | tf_op jit(solution)/shard_map/psum | solution.py:153
  135.8 1.3 dynamic-update-slice
  137.1 21.7 %all-reduce = f32[8]{0:T(128)S(1)} all-reduce(f32[8]{0:T(128)S(1)} %dynamic-update-slice), channel_id=1, replica_groups=mesh['grp'=2,'slab'=4,'orb'=2,'rep'=2] {'slab','orb'}, use_global_device_ids=true, to_apply=%add | all-reduce | flops 8 | bytes 64
  160.0 1.6 copy.39
  (80 shorter events, 13.4 us)
Async XLA Ops:
  7.2 152.8 %all-reduce.3.cloned.1.call-start = ((), (), s32[]{:S(2)}) async-start(), calls=%async_computation | async-start | bytes 262144 | tf_op jit(solution)/shard_map/psum | solution.py:153
  13.3 8.3 %collective-permute-start = (bf16[2,32,1024]{2,1,0:T(8,128)(2,1)S(1)}, bf16[2,32,1024]{2,1,0:T(8,128)(2,1)S(1)}, u32[]{:S(2)}, u32[]{:S(2)}) collective-permute-start(bf16[2,32,1024]{2,1,0:T(8,128)(2,1)S(1)} %all_gather.9), channel_id=1, source_target_pairs={{0,4},{4,8},{8,12},{12,0},{1,5},{5,9},{9,13},{13,1},{2,6},{6,10},{... | collective-permute-start | bytes 393224 | tf_op jit(solution)/shard_map/ppermute | solution.py:14
  15.4 7.2 %collective-permute-start.3 = (bf16[2,32,1024]{2,1,0:T(8,128)(2,1)S(1)}, bf16[2,32,1024]{2,1,0:T(8,128)(2,1)S(1)}, u32[]{:S(2)}, u32[]{:S(2)}) collective-permute-start(bf16[2,32,1024]{2,1,0:T(8,128)(2,1)S(1)} %all_gather.9), channel_id=1, source_target_pairs={{0,12},{4,0},{8,4},{12,8},{1,13},{5,1},{9,5},{13,9},{2,14},{6,2},{... | collective-permute-start | bytes 393224 | tf_op jit(solution)/shard_map/ppermute | solution.py:14
  21.7 7.2 %collective-permute-start.1 = (bf16[2,32,1024]{2,1,0:T(8,128)(2,1)S(1)}, bf16[2,32,1024]{2,1,0:T(8,128)(2,1)S(1)}, u32[]{:S(2)}, u32[]{:S(2)}) collective-permute-start(bf16[2,32,1024]{2,1,0:T(8,128)(2,1)S(1)} %collective-permute-done), channel_id=1, source_target_pairs={{0,4},{4,8},{8,12},{12,0},{1,5},{5,9},{9,13},{13,1},{2,6},{6,10},{... | collective-permute-start | bytes 393224 | tf_op jit(solution)/shard_map/ppermute | solution.py:14
  22.6 6.7 %collective-permute-start.4 = (bf16[2,32,1024]{2,1,0:T(8,128)(2,1)S(1)}, bf16[2,32,1024]{2,1,0:T(8,128)(2,1)S(1)}, u32[]{:S(2)}, u32[]{:S(2)}) collective-permute-start(bf16[2,32,1024]{2,1,0:T(8,128)(2,1)S(1)} %collective-permute-done.3), channel_id=1, source_target_pairs={{0,12},{4,0},{8,4},{12,8},{1,13},{5,1},{9,5},{13,9},{2,14},{6,2},{... | collective-permute-start | bytes 393224 | tf_op jit(solution)/shard_map/ppermute | solution.py:14
  28.9 7.9 %collective-permute-start.2 = (bf16[2,32,1024]{2,1,0:T(8,128)(2,1)S(1)}, bf16[2,32,1024]{2,1,0:T(8,128)(2,1)S(1)}, u32[]{:S(2)}, u32[]{:S(2)}) collective-permute-start(bf16[2,32,1024]{2,1,0:T(8,128)(2,1)S(1)} %collective-permute-done.1), channel_id=1, source_target_pairs={{0,4},{4,8},{8,12},{12,0},{1,5},{5,9},{9,13},{13,1},{2,6},{6,10},{... | collective-permute-start | bytes 393224 | tf_op jit(solution)/shard_map/ppermute | solution.py:14
  29.2 8.0 %collective-permute-start.5 = (bf16[2,32,1024]{2,1,0:T(8,128)(2,1)S(1)}, bf16[2,32,1024]{2,1,0:T(8,128)(2,1)S(1)}, u32[]{:S(2)}, u32[]{:S(2)}) collective-permute-start(bf16[2,32,1024]{2,1,0:T(8,128)(2,1)S(1)} %collective-permute-done.4), channel_id=1, source_target_pairs={{0,12},{4,0},{8,4},{12,8},{1,13},{5,1},{9,5},{13,9},{2,14},{6,2},{... | collective-permute-start | bytes 393224 | tf_op jit(solution)/shard_map/ppermute | solution.py:14
  37.3 94.3 %copy-start.4 = (u32[32]{0:T(128)S(1)}, u32[32]{0:T(128)}, u32[]{:S(2)}) copy-start(u32[32]{0:T(128)} %constant.316) | copy-start | bytes 388
  37.3 5.2 %copy-start.1 = (f32[32,1024]{1,0:T(8,128)S(1)}, f32[32,1024]{1,0:T(8,128)}, u32[]{:S(2)}) copy-start(f32[32,1024]{1,0:T(8,128)} %get-tuple-element.783) | copy-start | bytes 393220 | tf_op jit(solution)/shard_map/while
  37.4 5.2 %copy-start.3 = (bf16[1,32,1024]{2,1,0:T(8,128)(2,1)S(1)}, bf16[1,32,1024]{2,1,0:T(8,128)(2,1)}, u32[]{:S(2)}) copy-start(bf16[1,32,1024]{2,1,0:T(8,128)(2,1)} %get-tuple-element.779) | copy-start | bytes 196612 | tf_op jit(solution)/shard_map/while
  47.5 17.6 %copy-start = (f32[1024,1024]{1,0:T(8,128)S(1)}, f32[1024,1024]{1,0:T(8,128)}, u32[]{:S(2)}) copy-start(f32[1024,1024]{1,0:T(8,128)} %get-tuple-element.609) | copy-start | bytes 12582916 | tf_op jit(solution)/shard_map/while/body/eval_jaxpr/cond
  120.3 5.2 %copy-start.1 = (f32[32,1024]{1,0:T(8,128)S(1)}, f32[32,1024]{1,0:T(8,128)}, u32[]{:S(2)}) copy-start(f32[32,1024]{1,0:T(8,128)} %get-tuple-element.783) | copy-start | bytes 393220 | tf_op jit(solution)/shard_map/while
  120.4 5.2 %copy-start.3 = (bf16[1,32,1024]{2,1,0:T(8,128)(2,1)S(1)}, bf16[1,32,1024]{2,1,0:T(8,128)(2,1)}, u32[]{:S(2)}) copy-start(bf16[1,32,1024]{2,1,0:T(8,128)(2,1)} %get-tuple-element.779) | copy-start | bytes 196612 | tf_op jit(solution)/shard_map/while
  125.6 5.2 %copy-start.1 = (f32[32,1024]{1,0:T(8,128)S(1)}, f32[32,1024]{1,0:T(8,128)}, u32[]{:S(2)}) copy-start(f32[32,1024]{1,0:T(8,128)} %get-tuple-element.783) | copy-start | bytes 393220 | tf_op jit(solution)/shard_map/while
  125.6 5.2 %copy-start.3 = (bf16[1,32,1024]{2,1,0:T(8,128)(2,1)S(1)}, bf16[1,32,1024]{2,1,0:T(8,128)(2,1)}, u32[]{:S(2)}) copy-start(bf16[1,32,1024]{2,1,0:T(8,128)(2,1)} %get-tuple-element.779) | copy-start | bytes 196612 | tf_op jit(solution)/shard_map/while
  130.9 0.7 copy-start.2
Sparse Core Ops, SparseCore 0:
  131.7 19.1 all-reduce.2
